TPU v7x, 128 devices: a whole 4x4x4 slice. The times are simulated.
128 devices in a mesh: section: 8 (over x_hi, z), fsdp: 16 (over y, x_lo, core).
Axes of the slice: x: 4 (x_hi: 2, x_lo: 2; x = x_hi * 2 + x_lo), y: 4, z: 4, core: 2. Of those that a mesh axis runs over, the one named last changes fastest.
Arguments:
- hidden_in: bfloat16 [8, 16, 64, 1536], P(None, 'fsdp'), may hold values from -6 to 6
- norm_gain: float32 [2, 8, 1536], P(None, 'section'), may hold values from 0.25 to 1.75
- qkv_weight: bfloat16 [2, 8, 1536, 2048], P(None, 'section', 'fsdp'), may hold values from -0.15625 to 0.15625
- qkv_bias: float32 [2, 8, 2048], P(None, 'section'), may hold values from -30 to 30, as said below
- out_weight: bfloat16 [2, 8, 1536, 1536], P(None, 'section', 'fsdp'), may hold values from -0.15625 to 0.15625
Outputs:
- hidden_out: bfloat16 [8, 16, 64, 1536], P('section', 'fsdp')
Inputs may be any that keep to these rules, and one draw needn't show every extreme that they name: `qkv_bias`: entries of the query, key and value biases.
All inputs are finite; a program needn't handle non-finite values.
Results may differ from a plain program's by a relative error of at most 0.035.
Values may be sent and summed in bfloat16 or wider, within the bound.
A program may use at most 128 MiB of HBM per device.

v0:
```python
from functools import partial
import math

import jax
import jax.numpy as jnp
from jax import lax
from jax.sharding import PartitionSpec as P

HEADS = 12
KV_HEADS = 2
HEAD_DIM = 128


THETA = 1000000.0
EPS = 1.0


def as_sent(array):

    def short(part):
        return part.astype(jnp.bfloat16) if part.dtype == jnp.float32 else part

    return jax.tree.map(short, array)


def passed_along(block, axis, distance):
    devices = range(lax.axis_size(axis))
    route = [((i - distance) % len(devices), i) for i in devices]
    return lax.ppermute(block, axis, route)


def from_root(value, axis, source):
    kept = jnp.where(lax.axis_index(axis) == source, value, 0).astype(value.dtype)
    return lax.psum(kept, axis)


def rotate(tensor, cosine, sine_part):
    half_dim = tensor.shape[-1] // 2
    leading = tensor[..., :half_dim]
    second = tensor[..., half_dim:]
    return jnp.concatenate(
        [leading * cosine - second * sine_part, second * cosine + leading * sine_part], axis=-1
    )


def attend_layer(hidden, gain, w_qkv, bias, w_out):
    rows, length, width = hidden.shape
    group_size = HEADS // KV_HEADS
    kv_width = KV_HEADS * HEAD_DIM
    wide = hidden.astype(jnp.float32)
    inv_rms = lax.rsqrt(jnp.mean(wide * wide, axis=-1, keepdims=True) + EPS)
    normed = (wide * inv_rms * gain).astype(jnp.bfloat16)
    projected = (
        jnp.dot(normed.reshape(rows * length, width), w_qkv, preferred_element_type=jnp.float32)
        + bias
    )
    projected = projected.reshape(rows, length, width + 2 * kv_width)
    queries = projected[..., :width].reshape(rows, length, KV_HEADS, group_size, HEAD_DIM)
    key_rows = projected[..., width : width + kv_width].reshape(rows, length, KV_HEADS, HEAD_DIM)
    value_rows = (
        projected[..., width + kv_width :]
        .astype(jnp.bfloat16)
        .reshape(rows, length, KV_HEADS, HEAD_DIM)
    )
    half_dim = HEAD_DIM // 2
    frequency = jnp.exp(
        jnp.arange(half_dim, dtype=jnp.float32) * (-2.0 * math.log(THETA) / HEAD_DIM)
    )
    angles = jnp.arange(length, dtype=jnp.float32)[:, None] * frequency[None, :]
    cosine = jnp.cos(angles)
    sine_part = jnp.sin(angles)
    queries = rotate(queries, cosine[None, :, None, None, :], sine_part[None, :, None, None, :])
    key_rows = rotate(key_rows, cosine[None, :, None, :], sine_part[None, :, None, :])
    scores = jnp.einsum(
        "rqkgd,rpkd->rkgqp", queries, key_rows, precision=lax.Precision.HIGHEST
    ) / math.sqrt(HEAD_DIM)
    causal = jnp.arange(length)[:, None] >= jnp.arange(length)[None, :]
    scores = jnp.where(causal, scores, -1e30)
    row_max = jnp.max(scores, axis=-1, keepdims=True)
    weights = jnp.exp(scores - row_max)
    probability = (weights / jnp.sum(weights, axis=-1, keepdims=True)).astype(jnp.bfloat16)
    context = jnp.einsum(
        "rkgqp,rpkd->rqkgd", probability, value_rows, preferred_element_type=jnp.float32
    )
    context = context.reshape(rows, length, width).astype(jnp.bfloat16)
    update = jnp.dot(
        context.reshape(rows * length, width), w_out, preferred_element_type=jnp.float32
    )
    return (wide + update.reshape(rows, length, width)).astype(jnp.bfloat16)


def run_span(weight_pair, gain, bias, block_rows):
    return attend_layer(block_rows, gain, weight_pair[0], bias, weight_pair[1])


def vanish(block_rows):
    return jnp.zeros_like(block_rows)


def per_device(hidden_in, norm_gain, qkv_weight, qkv_bias, out_weight):
    sections = lax.axis_size("section")
    my_section = lax.axis_index("section")
    micro_count = hidden_in.shape[0]
    owned_count = micro_count // sections
    tick_count = 2 * micro_count + sections - 1
    span_gains = norm_gain[:, 0]
    biases = qkv_bias[:, 0]
    waiting = jnp.zeros_like(hidden_in)
    result = jnp.zeros_like(hidden_in)

    def make_tick(layers):
        branches = [vanish]
        for span_no in range(2):
            branches.append(
                partial(run_span, layers[span_no], span_gains[span_no], biases[span_no])
            )

        def advance(moment, state_pair):
            waiting, result = state_pair
            work_item = moment - my_section
            active = (work_item >= 0) & (work_item < 2 * micro_count)
            span_id = jnp.clip(work_item // micro_count, 0, 1)
            slot_id = jnp.mod(work_item, micro_count)
            entering = lax.dynamic_index_in_dim(hidden_in, slot_id, 0, keepdims=False)
            stored = lax.dynamic_index_in_dim(waiting, slot_id, 0, keepdims=False)
            block_in = jnp.where((span_id == 0) & (my_section == 0), entering, stored)
            selector = jnp.where(active, span_id + 1, 0)
            block_out = lax.switch(selector, branches, block_in)
            arrived = jax.tree.map(
                lambda part, own: part.astype(own.dtype),
                passed_along(as_sent(block_out), "section", 1),
                block_out,
            )
            sender = jnp.mod(my_section - 1, sections)
            sent_item = moment - sender
            accept = (
                (sent_item >= 0)
                & (sent_item < 2 * micro_count)
                & jnp.logical_not((sender == sections - 1) & (sent_item >= micro_count))
            )
            got_slot = jnp.mod(sent_item, micro_count)
            before = lax.dynamic_index_in_dim(waiting, got_slot, 0, keepdims=False)
            waiting = lax.dynamic_update_index_in_dim(
                waiting, jnp.where(accept, arrived, before), got_slot, 0
            )
            finish = moment - (sections - 1) - micro_count
            completed = (finish >= 0) & (finish < micro_count)
            final_slot = jnp.clip(finish, 0, micro_count - 1)
            previous = lax.dynamic_index_in_dim(result, final_slot, 0, keepdims=False)
            owned = completed & (my_section == sections - 1)
            result = lax.dynamic_update_index_in_dim(
                result, jnp.where(owned, block_out, previous), final_slot, 0
            )
            return (waiting, result)

        return advance

    gathered_qkv, gathered_out = (
        lax.all_gather(qkv_weight[:, 0], "fsdp", axis=1, tiled=True),
        lax.all_gather(out_weight[:, 0], "fsdp", axis=1, tiled=True),
    )
    layers = ((gathered_qkv[0], gathered_out[0]), (gathered_qkv[1], gathered_out[1]))
    state_pair = lax.fori_loop(0, tick_count, make_tick(layers), (waiting, result))
    waiting, result = state_pair
    result = from_root(result, "section", sections - 1)
    return lax.dynamic_slice_in_dim(result, my_section * owned_count, owned_count, 0)


def solution(mesh):
    in_specs = (
        P(None, "fsdp", None, None),
        P(None, "section", None),
        P(None, "section", "fsdp", None),
        P(None, "section", None),
        P(None, "section", "fsdp", None),
    )
    out_specs = P("section", "fsdp", None, None)
    return jax.shard_map(
        per_device, mesh=mesh, in_specs=in_specs, out_specs=out_specs, check_vma=False
    )
```

profile of v0, /device:TPU:100, one launch (start us, length us, event | category | flops | bytes accessed | tf_op | source)
XLA Modules:
  0.0 730.0 jit_solution(1567321203957885636)
XLA Ops:
  9.5 57.7 %all-gather.7.cloned.1.call-done = bf16[2,1,1536,1536]{3,2,1,0:T(8,128)(2,1)} async-done(((bf16[2,1,96,1536]{3,2,1,0:T(8,128)(2,1)}), bf16[2,1,1536,1536]{3,2,1,0:T(8,128)(2,1)}) %all-gather.7.cloned.1.call-update) | async-done | bytes 9437200 | tf_op jit(solution)/shard_map/all_gather | solution.py:160
  67.2 8.0 %slice_bitcast_fusion.2 = (bf16[1536,1536]{1,0:T(8,128)(2,1)}, bf16[1536,1536]{1,0:T(8,128)(2,1)}) fusion(bf16[2,1,1536,1536]{3,2,1,0:T(8,128)(2,1)} %all-gather.7.cloned.1.call-done), kind=kLoop, calls=%fused_computation.91 | loop fusion | bytes 18874368 | tf_op jit(solution)/shard_map/squeeze | solution.py:162
  75.2 66.5 %all-gather.5.cloned.1.call-done = bf16[2,1,1536,2048]{3,2,1,0:T(8,128)(2,1)} async-done(((bf16[2,1,96,2048]{3,2,1,0:T(8,128)(2,1)}), bf16[2,1,1536,2048]{3,2,1,0:T(8,128)(2,1)}) %all-gather.5.cloned.1.call-update) | async-done | bytes 12582928 | tf_op jit(solution)/shard_map/all_gather | solution.py:159
  141.7 10.6 %slice_bitcast_fusion = (bf16[1536,2048]{1,0:T(8,128)(2,1)}, bf16[1536,2048]{1,0:T(8,128)(2,1)}) fusion(bf16[2,1,1536,2048]{3,2,1,0:T(8,128)(2,1)} %all-gather.5.cloned.1.call-done), kind=kLoop, calls=%fused_computation.89 | loop fusion | bytes 25165824 | tf_op jit(solution)/shard_map/squeeze | solution.py:162
  154.8 475.7 %while.20 = (s32[]{:T(128)}, bf16[8,1,64,1536]{3,2,1,0:T(8,128)(2,1)}, bf16[8,1,64,1536]{3,2,1,0:T(8,128)(2,1)}, s32[]{:T(128)}, pred[]{:T(512)}, /*index=5*/s32...) while((s32[]{:T(128)}, ...), condition=%wide.region_10.11_spmd, body=%wide.region_0.10_spmd.sunk | while | flops 795089600 | bytes 21876164 | solution.py:163
  156.0 11.0 %collective-permute-start = (bf16[1,64,1536]{2,1,0:T(8,128)(2,1)S(1)}, bf16[1,64,1536]{2,1,0:T(8,128)(2,1)S(1)}, u32[]{:S(2)}, u32[]{:S(2)}) collective-permute-start(bf16[1,64,1536]{2,1,0:T(8,128)(2,1)S(1)} %get-tuple-element.828), channel_id=1, source_target_pairs={{112,0},{0,16},{16,32},{32,48},{48,64},{64,80},{80,96},{96,112},{1... | collective-permute-start | bytes 589832 | tf_op jit(solution)/shard_map/while/body/eval_jaxpr/ppermute | solution.py:29
  173.5 16.8 %collective-permute-start = (bf16[1,64,1536]{2,1,0:T(8,128)(2,1)S(1)}, bf16[1,64,1536]{2,1,0:T(8,128)(2,1)S(1)}, u32[]{:S(2)}, u32[]{:S(2)}) collective-permute-start(bf16[1,64,1536]{2,1,0:T(8,128)(2,1)S(1)} %get-tuple-element.828), channel_id=1, source_target_pairs={{112,0},{0,16},{16,32},{32,48},{48,64},{64,80},{80,96},{96,112},{1... | collective-permute-start | bytes 589832 | tf_op jit(solution)/shard_map/while/body/eval_jaxpr/ppermute | solution.py:29
  195.9 16.8 %collective-permute-start = (bf16[1,64,1536]{2,1,0:T(8,128)(2,1)S(1)}, bf16[1,64,1536]{2,1,0:T(8,128)(2,1)S(1)}, u32[]{:S(2)}, u32[]{:S(2)}) collective-permute-start(bf16[1,64,1536]{2,1,0:T(8,128)(2,1)S(1)} %get-tuple-element.828), channel_id=1, source_target_pairs={{112,0},{0,16},{16,32},{32,48},{48,64},{64,80},{80,96},{96,112},{1... | collective-permute-start | bytes 589832 | tf_op jit(solution)/shard_map/while/body/eval_jaxpr/ppermute | solution.py:29
  217.8 16.8 %collective-permute-start = (bf16[1,64,1536]{2,1,0:T(8,128)(2,1)S(1)}, bf16[1,64,1536]{2,1,0:T(8,128)(2,1)S(1)}, u32[]{:S(2)}, u32[]{:S(2)}) collective-permute-start(bf16[1,64,1536]{2,1,0:T(8,128)(2,1)S(1)} %get-tuple-element.828), channel_id=1, source_target_pairs={{112,0},{0,16},{16,32},{32,48},{48,64},{64,80},{80,96},{96,112},{1... | collective-permute-start | bytes 589832 | tf_op jit(solution)/shard_map/while/body/eval_jaxpr/ppermute | solution.py:29
  239.7 16.8 %collective-permute-start = (bf16[1,64,1536]{2,1,0:T(8,128)(2,1)S(1)}, bf16[1,64,1536]{2,1,0:T(8,128)(2,1)S(1)}, u32[]{:S(2)}, u32[]{:S(2)}) collective-permute-start(bf16[1,64,1536]{2,1,0:T(8,128)(2,1)S(1)} %get-tuple-element.828), channel_id=1, source_target_pairs={{112,0},{0,16},{16,32},{32,48},{48,64},{64,80},{80,96},{96,112},{1... | collective-permute-start | bytes 589832 | tf_op jit(solution)/shard_map/while/body/eval_jaxpr/ppermute | solution.py:29
  261.6 16.8 %collective-permute-start = (bf16[1,64,1536]{2,1,0:T(8,128)(2,1)S(1)}, bf16[1,64,1536]{2,1,0:T(8,128)(2,1)S(1)}, u32[]{:S(2)}, u32[]{:S(2)}) collective-permute-start(bf16[1,64,1536]{2,1,0:T(8,128)(2,1)S(1)} %get-tuple-element.828), channel_id=1, source_target_pairs={{112,0},{0,16},{16,32},{32,48},{48,64},{64,80},{80,96},{96,112},{1... | collective-permute-start | bytes 589832 | tf_op jit(solution)/shard_map/while/body/eval_jaxpr/ppermute | solution.py:29
  283.6 16.8 %collective-permute-start = (bf16[1,64,1536]{2,1,0:T(8,128)(2,1)S(1)}, bf16[1,64,1536]{2,1,0:T(8,128)(2,1)S(1)}, u32[]{:S(2)}, u32[]{:S(2)}) collective-permute-start(bf16[1,64,1536]{2,1,0:T(8,128)(2,1)S(1)} %get-tuple-element.828), channel_id=1, source_target_pairs={{112,0},{0,16},{16,32},{32,48},{48,64},{64,80},{80,96},{96,112},{1... | collective-permute-start | bytes 589832 | tf_op jit(solution)/shard_map/while/body/eval_jaxpr/ppermute | solution.py:29
  305.4 10.7 %conditional.2 = (bf16[1,64,1536]{2,1,0:T(8,128)(2,1)S(1)}) conditional(s32[]{:T(128)} %clamp.15, () %tuple.78, (bf16[1,64,1536]{2,1,0:T(8,128)(2,1)S(1)}, f32[1,1536]{1,0:T(1,128)S(1)}, bf16[1536,2048]{1,0:T(8,128)(2,1)}, f32[1,2048]{1,0:T(1,128)S(1)}, bf16[1536,1536]{1,0:T(8,128)(2,1)}) %tuple.79, ...), branch_computations={%region_1.1_spmd, %region_2.5_spmd, %region_6.9_spmd} | conditional | flops 794794624 | bytes 18532876 | solution.py:128
  316.1 6.2 collective-permute-start
  327.3 10.7 %conditional.2 = (bf16[1,64,1536]{2,1,0:T(8,128)(2,1)S(1)}) conditional(s32[]{:T(128)} %clamp.15, () %tuple.78, (bf16[1,64,1536]{2,1,0:T(8,128)(2,1)S(1)}, f32[1,1536]{1,0:T(1,128)S(1)}, bf16[1536,2048]{1,0:T(8,128)(2,1)}, f32[1,2048]{1,0:T(1,128)S(1)}, bf16[1536,1536]{1,0:T(8,128)(2,1)}) %tuple.79, ...), branch_computations={%region_1.1_spmd, %region_2.5_spmd, %region_6.9_spmd} | conditional | flops 794794624 | bytes 18532876 | solution.py:128
  349.2 10.7 %conditional.2 = (bf16[1,64,1536]{2,1,0:T(8,128)(2,1)S(1)}) conditional(s32[]{:T(128)} %clamp.15, () %tuple.78, (bf16[1,64,1536]{2,1,0:T(8,128)(2,1)S(1)}, f32[1,1536]{1,0:T(1,128)S(1)}, bf16[1536,2048]{1,0:T(8,128)(2,1)}, f32[1,2048]{1,0:T(1,128)S(1)}, bf16[1536,1536]{1,0:T(8,128)(2,1)}) %tuple.79, ...), branch_computations={%region_1.1_spmd, %region_2.5_spmd, %region_6.9_spmd} | conditional | flops 794794624 | bytes 18532876 | solution.py:128
  371.1 10.7 %conditional.2 = (bf16[1,64,1536]{2,1,0:T(8,128)(2,1)S(1)}) conditional(s32[]{:T(128)} %clamp.15, () %tuple.78, (bf16[1,64,1536]{2,1,0:T(8,128)(2,1)S(1)}, f32[1,1536]{1,0:T(1,128)S(1)}, bf16[1536,2048]{1,0:T(8,128)(2,1)}, f32[1,2048]{1,0:T(1,128)S(1)}, bf16[1536,1536]{1,0:T(8,128)(2,1)}) %tuple.79, ...), branch_computations={%region_1.1_spmd, %region_2.5_spmd, %region_6.9_spmd} | conditional | flops 794794624 | bytes 18532876 | solution.py:128
  381.8 6.2 collective-permute-start
  393.0 10.7 %conditional.2 = (bf16[1,64,1536]{2,1,0:T(8,128)(2,1)S(1)}) conditional(s32[]{:T(128)} %clamp.15, () %tuple.78, (bf16[1,64,1536]{2,1,0:T(8,128)(2,1)S(1)}, f32[1,1536]{1,0:T(1,128)S(1)}, bf16[1536,2048]{1,0:T(8,128)(2,1)}, f32[1,2048]{1,0:T(1,128)S(1)}, bf16[1536,1536]{1,0:T(8,128)(2,1)}) %tuple.79, ...), branch_computations={%region_1.1_spmd, %region_2.5_spmd, %region_6.9_spmd} | conditional | flops 794794624 | bytes 18532876 | solution.py:128
  414.9 10.7 %conditional.2 = (bf16[1,64,1536]{2,1,0:T(8,128)(2,1)S(1)}) conditional(s32[]{:T(128)} %clamp.15, () %tuple.78, (bf16[1,64,1536]{2,1,0:T(8,128)(2,1)S(1)}, f32[1,1536]{1,0:T(1,128)S(1)}, bf16[1536,2048]{1,0:T(8,128)(2,1)}, f32[1,2048]{1,0:T(1,128)S(1)}, bf16[1536,1536]{1,0:T(8,128)(2,1)}) %tuple.79, ...), branch_computations={%region_1.1_spmd, %region_2.5_spmd, %region_6.9_spmd} | conditional | flops 794794624 | bytes 18532876 | solution.py:128
  436.8 10.7 %conditional.2 = (bf16[1,64,1536]{2,1,0:T(8,128)(2,1)S(1)}) conditional(s32[]{:T(128)} %clamp.15, () %tuple.78, (bf16[1,64,1536]{2,1,0:T(8,128)(2,1)S(1)}, f32[1,1536]{1,0:T(1,128)S(1)}, bf16[1536,2048]{1,0:T(8,128)(2,1)}, f32[1,2048]{1,0:T(1,128)S(1)}, bf16[1536,1536]{1,0:T(8,128)(2,1)}) %tuple.79, ...), branch_computations={%region_1.1_spmd, %region_2.5_spmd, %region_6.9_spmd} | conditional | flops 794794624 | bytes 18532876 | solution.py:128
  458.7 10.7 %conditional.2 = (bf16[1,64,1536]{2,1,0:T(8,128)(2,1)S(1)}) conditional(s32[]{:T(128)} %clamp.15, () %tuple.78, (bf16[1,64,1536]{2,1,0:T(8,128)(2,1)S(1)}, f32[1,1536]{1,0:T(1,128)S(1)}, bf16[1536,2048]{1,0:T(8,128)(2,1)}, f32[1,2048]{1,0:T(1,128)S(1)}, bf16[1536,1536]{1,0:T(8,128)(2,1)}) %tuple.79, ...), branch_computations={%region_1.1_spmd, %region_2.5_spmd, %region_6.9_spmd} | conditional | flops 794794624 | bytes 18532876 | solution.py:128
  480.6 10.7 %conditional.2 = (bf16[1,64,1536]{2,1,0:T(8,128)(2,1)S(1)}) conditional(s32[]{:T(128)} %clamp.15, () %tuple.78, (bf16[1,64,1536]{2,1,0:T(8,128)(2,1)S(1)}, f32[1,1536]{1,0:T(1,128)S(1)}, bf16[1536,2048]{1,0:T(8,128)(2,1)}, f32[1,2048]{1,0:T(1,128)S(1)}, bf16[1536,1536]{1,0:T(8,128)(2,1)}) %tuple.79, ...), branch_computations={%region_1.1_spmd, %region_2.5_spmd, %region_6.9_spmd} | conditional | flops 794794624 | bytes 18532876 | solution.py:128
  491.3 6.2 collective-permute-start
  502.5 10.7 %conditional.2 = (bf16[1,64,1536]{2,1,0:T(8,128)(2,1)S(1)}) conditional(s32[]{:T(128)} %clamp.15, () %tuple.78, (bf16[1,64,1536]{2,1,0:T(8,128)(2,1)S(1)}, f32[1,1536]{1,0:T(1,128)S(1)}, bf16[1536,2048]{1,0:T(8,128)(2,1)}, f32[1,2048]{1,0:T(1,128)S(1)}, bf16[1536,1536]{1,0:T(8,128)(2,1)}) %tuple.79, ...), branch_computations={%region_1.1_spmd, %region_2.5_spmd, %region_6.9_spmd} | conditional | flops 794794624 | bytes 18532876 | solution.py:128
  521.8 10.7 %conditional.2 = (bf16[1,64,1536]{2,1,0:T(8,128)(2,1)S(1)}) conditional(s32[]{:T(128)} %clamp.15, () %tuple.78, (bf16[1,64,1536]{2,1,0:T(8,128)(2,1)S(1)}, f32[1,1536]{1,0:T(1,128)S(1)}, bf16[1536,2048]{1,0:T(8,128)(2,1)}, f32[1,2048]{1,0:T(1,128)S(1)}, bf16[1536,1536]{1,0:T(8,128)(2,1)}) %tuple.79, ...), branch_computations={%region_1.1_spmd, %region_2.5_spmd, %region_6.9_spmd} | conditional | flops 794794624 | bytes 18532876 | solution.py:128
  540.3 10.7 %conditional.2 = (bf16[1,64,1536]{2,1,0:T(8,128)(2,1)S(1)}) conditional(s32[]{:T(128)} %clamp.15, () %tuple.78, (bf16[1,64,1536]{2,1,0:T(8,128)(2,1)S(1)}, f32[1,1536]{1,0:T(1,128)S(1)}, bf16[1536,2048]{1,0:T(8,128)(2,1)}, f32[1,2048]{1,0:T(1,128)S(1)}, bf16[1536,1536]{1,0:T(8,128)(2,1)}) %tuple.79, ...), branch_computations={%region_1.1_spmd, %region_2.5_spmd, %region_6.9_spmd} | conditional | flops 794794624 | bytes 18532876 | solution.py:128
  558.6 10.7 %conditional.2 = (bf16[1,64,1536]{2,1,0:T(8,128)(2,1)S(1)}) conditional(s32[]{:T(128)} %clamp.15, () %tuple.78, (bf16[1,64,1536]{2,1,0:T(8,128)(2,1)S(1)}, f32[1,1536]{1,0:T(1,128)S(1)}, bf16[1536,2048]{1,0:T(8,128)(2,1)}, f32[1,2048]{1,0:T(1,128)S(1)}, bf16[1536,1536]{1,0:T(8,128)(2,1)}) %tuple.79, ...), branch_computations={%region_1.1_spmd, %region_2.5_spmd, %region_6.9_spmd} | conditional | flops 794794624 | bytes 18532876 | solution.py:128
  576.9 10.7 %conditional.2 = (bf16[1,64,1536]{2,1,0:T(8,128)(2,1)S(1)}) conditional(s32[]{:T(128)} %clamp.15, () %tuple.78, (bf16[1,64,1536]{2,1,0:T(8,128)(2,1)S(1)}, f32[1,1536]{1,0:T(1,128)S(1)}, bf16[1536,2048]{1,0:T(8,128)(2,1)}, f32[1,2048]{1,0:T(1,128)S(1)}, bf16[1536,1536]{1,0:T(8,128)(2,1)}) %tuple.79, ...), branch_computations={%region_1.1_spmd, %region_2.5_spmd, %region_6.9_spmd} | conditional | flops 794794624 | bytes 18532876 | solution.py:128
  595.2 10.7 %conditional.2 = (bf16[1,64,1536]{2,1,0:T(8,128)(2,1)S(1)}) conditional(s32[]{:T(128)} %clamp.15, () %tuple.78, (bf16[1,64,1536]{2,1,0:T(8,128)(2,1)S(1)}, f32[1,1536]{1,0:T(1,128)S(1)}, bf16[1536,2048]{1,0:T(8,128)(2,1)}, f32[1,2048]{1,0:T(1,128)S(1)}, bf16[1536,1536]{1,0:T(8,128)(2,1)}) %tuple.79, ...), branch_computations={%region_1.1_spmd, %region_2.5_spmd, %region_6.9_spmd} | conditional | flops 794794624 | bytes 18532876 | solution.py:128
  613.5 10.7 %conditional.2 = (bf16[1,64,1536]{2,1,0:T(8,128)(2,1)S(1)}) conditional(s32[]{:T(128)} %clamp.15, () %tuple.78, (bf16[1,64,1536]{2,1,0:T(8,128)(2,1)S(1)}, f32[1,1536]{1,0:T(1,128)S(1)}, bf16[1536,2048]{1,0:T(8,128)(2,1)}, f32[1,2048]{1,0:T(1,128)S(1)}, bf16[1536,1536]{1,0:T(8,128)(2,1)}) %tuple.79, ...), branch_computations={%region_1.1_spmd, %region_2.5_spmd, %region_6.9_spmd} | conditional | flops 794794624 | bytes 18532876 | solution.py:128
  633.3 88.6 %all-reduce.2.cloned.1.call-done = bf16[8,1,64,1536]{3,2,1,0:T(8,128)(2,1)} async-done(((bf16[8,1,64,1536]{3,2,1,0:T(8,128)(2,1)}), bf16[8,1,64,1536]{3,2,1,0:T(8,128)(2,1)}) %all-reduce.2.cloned.1.call-update) | async-done | bytes 1572880 | tf_op jit(solution)/shard_map/psum | solution.py:34
  (522 shorter events, 352.2 us)
Async XLA Ops:
  6.5 60.7 %all-gather.7.cloned.1.call-start = ((), (), s32[]{:S(2)}) async-start(), calls=%async_computation.2 | async-start | bytes 10027008 | tf_op jit(solution)/shard_map/all_gather | solution.py:160
  7.3 134.4 %all-gather.5.cloned.1.call-start = ((), (), s32[]{:S(2)}) async-start(), calls=%async_computation.1 | async-start | bytes 13369344 | tf_op jit(solution)/shard_map/all_gather | solution.py:159
  8.0 713.9 %all-reduce.2.cloned.1.call-start = ((), (), s32[]{:S(2)}) async-start(), calls=%async_computation | async-start | bytes 3145728 | tf_op jit(solution)/shard_map/psum | solution.py:34
  156.0 15.5 %collective-permute-start = (bf16[1,64,1536]{2,1,0:T(8,128)(2,1)S(1)}, bf16[1,64,1536]{2,1,0:T(8,128)(2,1)S(1)}, u32[]{:S(2)}, u32[]{:S(2)}) collective-permute-start(bf16[1,64,1536]{2,1,0:T(8,128)(2,1)S(1)} %get-tuple-element.828), channel_id=1, source_target_pairs={{112,0},{0,16},{16,32},{32,48},{48,64},{64,80},{80,96},{96,112},{1... | collective-permute-start | bytes 589832 | tf_op jit(solution)/shard_map/while/body/eval_jaxpr/ppermute | solution.py:29
  173.5 20.5 %collective-permute-start = (bf16[1,64,1536]{2,1,0:T(8,128)(2,1)S(1)}, bf16[1,64,1536]{2,1,0:T(8,128)(2,1)S(1)}, u32[]{:S(2)}, u32[]{:S(2)}) collective-permute-start(bf16[1,64,1536]{2,1,0:T(8,128)(2,1)S(1)} %get-tuple-element.828), channel_id=1, source_target_pairs={{112,0},{0,16},{16,32},{32,48},{48,64},{64,80},{80,96},{96,112},{1... | collective-permute-start | bytes 589832 | tf_op jit(solution)/shard_map/while/body/eval_jaxpr/ppermute | solution.py:29
  195.9 20.0 %collective-permute-start = (bf16[1,64,1536]{2,1,0:T(8,128)(2,1)S(1)}, bf16[1,64,1536]{2,1,0:T(8,128)(2,1)S(1)}, u32[]{:S(2)}, u32[]{:S(2)}) collective-permute-start(bf16[1,64,1536]{2,1,0:T(8,128)(2,1)S(1)} %get-tuple-element.828), channel_id=1, source_target_pairs={{112,0},{0,16},{16,32},{32,48},{48,64},{64,80},{80,96},{96,112},{1... | collective-permute-start | bytes 589832 | tf_op jit(solution)/shard_map/while/body/eval_jaxpr/ppermute | solution.py:29
  217.8 20.0 %collective-permute-start = (bf16[1,64,1536]{2,1,0:T(8,128)(2,1)S(1)}, bf16[1,64,1536]{2,1,0:T(8,128)(2,1)S(1)}, u32[]{:S(2)}, u32[]{:S(2)}) collective-permute-start(bf16[1,64,1536]{2,1,0:T(8,128)(2,1)S(1)} %get-tuple-element.828), channel_id=1, source_target_pairs={{112,0},{0,16},{16,32},{32,48},{48,64},{64,80},{80,96},{96,112},{1... | collective-permute-start | bytes 589832 | tf_op jit(solution)/shard_map/while/body/eval_jaxpr/ppermute | solution.py:29
  239.7 20.0 %collective-permute-start = (bf16[1,64,1536]{2,1,0:T(8,128)(2,1)S(1)}, bf16[1,64,1536]{2,1,0:T(8,128)(2,1)S(1)}, u32[]{:S(2)}, u32[]{:S(2)}) collective-permute-start(bf16[1,64,1536]{2,1,0:T(8,128)(2,1)S(1)} %get-tuple-element.828), channel_id=1, source_target_pairs={{112,0},{0,16},{16,32},{32,48},{48,64},{64,80},{80,96},{96,112},{1... | collective-permute-start | bytes 589832 | tf_op jit(solution)/shard_map/while/body/eval_jaxpr/ppermute | solution.py:29
  261.6 20.0 %collective-permute-start = (bf16[1,64,1536]{2,1,0:T(8,128)(2,1)S(1)}, bf16[1,64,1536]{2,1,0:T(8,128)(2,1)S(1)}, u32[]{:S(2)}, u32[]{:S(2)}) collective-permute-start(bf16[1,64,1536]{2,1,0:T(8,128)(2,1)S(1)} %get-tuple-element.828), channel_id=1, source_target_pairs={{112,0},{0,16},{16,32},{32,48},{48,64},{64,80},{80,96},{96,112},{1... | collective-permute-start | bytes 589832 | tf_op jit(solution)/shard_map/while/body/eval_jaxpr/ppermute | solution.py:29
  283.6 20.0 %collective-permute-start = (bf16[1,64,1536]{2,1,0:T(8,128)(2,1)S(1)}, bf16[1,64,1536]{2,1,0:T(8,128)(2,1)S(1)}, u32[]{:S(2)}, u32[]{:S(2)}) collective-permute-start(bf16[1,64,1536]{2,1,0:T(8,128)(2,1)S(1)} %get-tuple-element.828), channel_id=1, source_target_pairs={{112,0},{0,16},{16,32},{32,48},{48,64},{64,80},{80,96},{96,112},{1... | collective-permute-start | bytes 589832 | tf_op jit(solution)/shard_map/while/body/eval_jaxpr/ppermute | solution.py:29
  316.1 9.4 %collective-permute-start = (bf16[1,64,1536]{2,1,0:T(8,128)(2,1)S(1)}, bf16[1,64,1536]{2,1,0:T(8,128)(2,1)S(1)}, u32[]{:S(2)}, u32[]{:S(2)}) collective-permute-start(bf16[1,64,1536]{2,1,0:T(8,128)(2,1)S(1)} %get-tuple-element.828), channel_id=1, source_target_pairs={{112,0},{0,16},{16,32},{32,48},{48,64},{64,80},{80,96},{96,112},{1... | collective-permute-start | bytes 589832 | tf_op jit(solution)/shard_map/while/body/eval_jaxpr/ppermute | solution.py:29
  338.0 9.4 %collective-permute-start = (bf16[1,64,1536]{2,1,0:T(8,128)(2,1)S(1)}, bf16[1,64,1536]{2,1,0:T(8,128)(2,1)S(1)}, u32[]{:S(2)}, u32[]{:S(2)}) collective-permute-start(bf16[1,64,1536]{2,1,0:T(8,128)(2,1)S(1)} %get-tuple-element.828), channel_id=1, source_target_pairs={{112,0},{0,16},{16,32},{32,48},{48,64},{64,80},{80,96},{96,112},{1... | collective-permute-start | bytes 589832 | tf_op jit(solution)/shard_map/while/body/eval_jaxpr/ppermute | solution.py:29
  359.9 9.3 %collective-permute-start = (bf16[1,64,1536]{2,1,0:T(8,128)(2,1)S(1)}, bf16[1,64,1536]{2,1,0:T(8,128)(2,1)S(1)}, u32[]{:S(2)}, u32[]{:S(2)}) collective-permute-start(bf16[1,64,1536]{2,1,0:T(8,128)(2,1)S(1)} %get-tuple-element.828), channel_id=1, source_target_pairs={{112,0},{0,16},{16,32},{32,48},{48,64},{64,80},{80,96},{96,112},{1... | collective-permute-start | bytes 589832 | tf_op jit(solution)/shard_map/while/body/eval_jaxpr/ppermute | solution.py:29
  381.8 9.4 %collective-permute-start = (bf16[1,64,1536]{2,1,0:T(8,128)(2,1)S(1)}, bf16[1,64,1536]{2,1,0:T(8,128)(2,1)S(1)}, u32[]{:S(2)}, u32[]{:S(2)}) collective-permute-start(bf16[1,64,1536]{2,1,0:T(8,128)(2,1)S(1)} %get-tuple-element.828), channel_id=1, source_target_pairs={{112,0},{0,16},{16,32},{32,48},{48,64},{64,80},{80,96},{96,112},{1... | collective-permute-start | bytes 589832 | tf_op jit(solution)/shard_map/while/body/eval_jaxpr/ppermute | solution.py:29
  403.7 9.3 %collective-permute-start = (bf16[1,64,1536]{2,1,0:T(8,128)(2,1)S(1)}, bf16[1,64,1536]{2,1,0:T(8,128)(2,1)S(1)}, u32[]{:S(2)}, u32[]{:S(2)}) collective-permute-start(bf16[1,64,1536]{2,1,0:T(8,128)(2,1)S(1)} %get-tuple-element.828), channel_id=1, source_target_pairs={{112,0},{0,16},{16,32},{32,48},{48,64},{64,80},{80,96},{96,112},{1... | collective-permute-start | bytes 589832 | tf_op jit(solution)/shard_map/while/body/eval_jaxpr/ppermute | solution.py:29
  425.6 9.3 %collective-permute-start = (bf16[1,64,1536]{2,1,0:T(8,128)(2,1)S(1)}, bf16[1,64,1536]{2,1,0:T(8,128)(2,1)S(1)}, u32[]{:S(2)}, u32[]{:S(2)}) collective-permute-start(bf16[1,64,1536]{2,1,0:T(8,128)(2,1)S(1)} %get-tuple-element.828), channel_id=1, source_target_pairs={{112,0},{0,16},{16,32},{32,48},{48,64},{64,80},{80,96},{96,112},{1... | collective-permute-start | bytes 589832 | tf_op jit(solution)/shard_map/while/body/eval_jaxpr/ppermute | solution.py:29
  447.5 9.4 %collective-permute-start = (bf16[1,64,1536]{2,1,0:T(8,128)(2,1)S(1)}, bf16[1,64,1536]{2,1,0:T(8,128)(2,1)S(1)}, u32[]{:S(2)}, u32[]{:S(2)}) collective-permute-start(bf16[1,64,1536]{2,1,0:T(8,128)(2,1)S(1)} %get-tuple-element.828), channel_id=1, source_target_pairs={{112,0},{0,16},{16,32},{32,48},{48,64},{64,80},{80,96},{96,112},{1... | collective-permute-start | bytes 589832 | tf_op jit(solution)/shard_map/while/body/eval_jaxpr/ppermute | solution.py:29
  469.4 9.3 %collective-permute-start = (bf16[1,64,1536]{2,1,0:T(8,128)(2,1)S(1)}, bf16[1,64,1536]{2,1,0:T(8,128)(2,1)S(1)}, u32[]{:S(2)}, u32[]{:S(2)}) collective-permute-start(bf16[1,64,1536]{2,1,0:T(8,128)(2,1)S(1)} %get-tuple-element.828), channel_id=1, source_target_pairs={{112,0},{0,16},{16,32},{32,48},{48,64},{64,80},{80,96},{96,112},{1... | collective-permute-start | bytes 589832 | tf_op jit(solution)/shard_map/while/body/eval_jaxpr/ppermute | solution.py:29
  491.3 9.4 %collective-permute-start = (bf16[1,64,1536]{2,1,0:T(8,128)(2,1)S(1)}, bf16[1,64,1536]{2,1,0:T(8,128)(2,1)S(1)}, u32[]{:S(2)}, u32[]{:S(2)}) collective-permute-start(bf16[1,64,1536]{2,1,0:T(8,128)(2,1)S(1)} %get-tuple-element.828), channel_id=1, source_target_pairs={{112,0},{0,16},{16,32},{32,48},{48,64},{64,80},{80,96},{96,112},{1... | collective-permute-start | bytes 589832 | tf_op jit(solution)/shard_map/while/body/eval_jaxpr/ppermute | solution.py:29
  513.2 6.8 collective-permute-start
  532.5 5.9 collective-permute-start
  551.0 5.7 collective-permute-start
  569.3 5.7 collective-permute-start
  587.5 5.7 collective-permute-start
  605.8 5.7 collective-permute-start
  624.1 5.7 collective-permute-start
Sparse Core Ops, SparseCore 0:
  9.0 58.1 all-gather.6
  68.9 72.7 all-gather.4
  633.4 88.4 all-reduce.1
where the time goes:
time: 737 us; the launch traced here: 730 us
  waiting for transfers between devices  269 us (36%)
  starting transfers between devices  168 us (23%)
  matrix products  143 us (19%)
  other arithmetic  73.9 us (10%)
  local copies, waits for them, and re-layouts  60.4 us (8%)
  between operations  13.1 us (2%)
    ppermute x23, starting transfers between devices, passed_along(): return lax.ppermute(block, axis, route)  168 us
    psum x1, waiting for transfers between devices, from_root(): return lax.psum(kept, axis)  88.6 us
    all_gather x1, waiting for transfers between devices, per_device(): lax.all_gather(qkv_weight[:, 0], 'fsdp', axis=1, tiled=True)  66.5 us
    dot_general x16, matrix products, attend_layer(): jnp.dot(normed.reshape(rows * length, width), w_qkv, preferred_element_ty...  64.7 us
    all_gather x1, waiting for transfers between devices, per_device(): lax.all_gather(out_weight[:, 0], 'fsdp', axis=1, tiled=True)  57.7 us
    ppermute x23, waiting for transfers between devices, passed_along(): return lax.ppermute(block, axis, route)  54.7 us
    dot_general x16, matrix products, attend_layer(): jnp.dot(context.reshape(rows * length, width), w_out, preferred_element_t...  52.2 us
    dynamic_slice x23, other arithmetic, advance(): before = lax.dynamic_index_in_dim(waiting, got_slot, 0, keepdims=False)  26.4 us
  transfers between devices with their start and end apart: 26, of which 26 were waited for; matrix products, arithmetic and copies ran while one was open for 7% of the time, Pallas kernels for 0%

commit v1 on v0

v1 whole, which is shorter than its diff:
```python
import functools
import math

import jax
import jax.numpy as jnp
import numpy as np
from jax import lax
from jax.experimental import pallas as pl
from jax.experimental.pallas import tpu as pltpu
from jax.sharding import PartitionSpec as P

HEADS = 12
KV_HEADS = 2
HEAD_DIM = 128
GROUP = HEADS // KV_HEADS
LEN = 64
D = HEADS * HEAD_DIM
QKV = D + 2 * KV_HEADS * HEAD_DIM
SECTIONS = 8
FSDP = 16
ROWS = D // FSDP
HALF = ROWS // 2
MICRO = 8
STEPS = 2 * MICRO
CHUNKS = 3
CW = D // CHUNKS
FINAL = STEPS
THETA = 1000000.0
EPS = 1.0
EVENTS = 16
MESH = pl.DeviceIdType.MESH


def tables():
    frequency = np.exp(np.arange(HEAD_DIM // 2) * (-2.0 * math.log(THETA) / HEAD_DIM))
    angles = np.arange(LEN)[:, None] * frequency[None, :]
    cosine, sine = np.cos(angles), np.sin(angles)
    full_cos = np.concatenate([cosine, cosine], axis=1)
    full_sin = np.concatenate([-sine, sine], axis=1)
    scale = 1.0 / math.sqrt(HEAD_DIM)
    mask = np.where(np.arange(LEN)[:, None] >= np.arange(LEN)[None, :], 0.0, -1e30)
    rope = np.stack([full_cos * scale, full_sin * scale, full_cos, full_sin])
    return rope.astype(np.float32), mask.astype(np.float32)


def split_two(value):
    high = value.astype(jnp.bfloat16)
    low = (value - high.astype(jnp.float32)).astype(jnp.bfloat16)
    return high, low


def kernel(
    hidden_hbm,
    gain_ref,
    qkv_hbm,
    bias_ref,
    out_hbm,
    rope_ref,
    mask_ref,
    result_ref,
    wq,
    wo,
    inbox,
    outbox,
    acc,
    ctx,
    own_sem,
    gsend,
    grecv,
    hsend,
    hrecv,
):
    s = lax.axis_index("section")
    f = lax.axis_index("fsdp")
    y = lax.div(f, 4)
    low = lax.rem(f, 4)
    x = lax.div(low, 2)
    core = lax.rem(f, 2)
    mirrored = f + 2 - 4 * x
    x_other = low + 2 - 4 * x
    y_next = lax.rem(y + 1, 4) * 4
    y_prev = lax.rem(y + 3, 4) * 4
    y_far = lax.rem(y + 2, 4) * 4
    flip = 1 - 2 * core

    dev_next = y_next + low
    dev_prev = y_prev + low
    dev_x = mirrored
    dev_sib = f + flip

    blocks = (
        f,
        y_prev + low,
        y_next + low,
        mirrored,
        y_far + low,
        y_prev + x_other,
        y_next + x_other,
        y_far + x_other,
    )
    OWN, PREV, NEXT, ACROSS, FAR, XPREV, XNEXT, XFAR = blocks

    tensors = ((wq, 0), (wo, 0), (wq, 1), (wo, 1))
    sources = ((qkv_hbm, 0), (out_hbm, 0), (qkv_hbm, 1), (out_hbm, 1))

    def region(t, block, first=0, count=ROWS):
        ref, layer = tensors[t]
        start = pl.multiple_of(block * ROWS + first, 16)
        return ref.at[layer, pl.ds(start, count), :]

    sends = {
        0: (OWN, 0, ROWS, dev_next),
        1: (OWN, 0, ROWS, dev_prev),
        2: (OWN, 0, ROWS, dev_x),
        3: (PREV, 0, HALF, dev_next),
        4: (NEXT, HALF, HALF, dev_prev),
        5: (ACROSS, 0, ROWS, dev_next),
        6: (ACROSS, 0, ROWS, dev_prev),
        7: (FAR, 0, ROWS, dev_x),
    }
    lands = {
        0: (PREV, 0, ROWS),
        1: (NEXT, 0, ROWS),
        2: (ACROSS, 0, ROWS),
        3: (FAR, 0, HALF),
        4: (FAR, HALF, HALF),
        5: (XPREV, 0, ROWS),
        6: (XNEXT, 0, ROWS),
        7: (XFAR, 0, ROWS),
    }
    for n in range(8):
        sends[8 + n] = (blocks[n], 0, ROWS, dev_sib)
        lands[8 + n] = (blocks[n] + flip, 0, ROWS)

    def outgoing(t, e):
        block, first, count, target = sends[e]
        part = region(t, block, first, count)
        return pltpu.make_async_remote_copy(
            src_ref=part,
            dst_ref=part,
            send_sem=gsend.at[t, e],
            recv_sem=grecv.at[t, e],
            device_id=(s, target),
            device_id_type=MESH,
        )

    def arrived(t, e):
        block, first, count = lands[e]
        part = region(t, block, first, count)
        pltpu.make_async_remote_copy(
            src_ref=part,
            dst_ref=part,
            send_sem=gsend.at[t, e],
            recv_sem=grecv.at[t, e],
            device_id=(s, dev_sib),
            device_id_type=MESH,
        ).wait_recv()

    def own_copy(t):
        ref, layer = sources[t]
        return pltpu.make_async_copy(ref.at[layer, 0], region(t, OWN), own_sem.at[t])

    def gather_a(t):
        own_copy(t).wait()
        for e in (0, 1, 2, 8):
            outgoing(t, e).start()

    def gather_b(t):
        for e, then in ((0, (3, 9)), (1, (4, 10)), (2, (5, 6, 11))):
            arrived(t, e)
            for n in then:
                outgoing(t, n).start()

    def gather_c(t):
        arrived(t, 3)
        arrived(t, 4)
        for n in (7, 12):
            outgoing(t, n).start()
        arrived(t, 5)
        outgoing(t, 13).start()
        arrived(t, 6)
        outgoing(t, 14).start()

    def gather_d(t):
        arrived(t, 7)
        outgoing(t, 15).start()
        for e in range(8, 16):
            arrived(t, e)

    def entering(k, j):
        return pltpu.make_async_copy(
            hidden_hbm.at[k, 0, :, pl.ds(j * CW, CW)], inbox.at[k, j], hrecv.at[k, j]
        )

    for t in range(4):
        own_copy(t).start()

    @pl.when(s == 0)
    def _():
        for k in range(MICRO):
            for j in range(CHUNKS):
                entering(k, j).start()

    crossing_in = (s == 4) | (s == 0)
    crossing_out = (s == 3) | (s == SECTIONS - 1)
    before = (lax.rem(s + SECTIONS - 1, SECTIONS), jnp.where(crossing_in, mirrored, f))
    after_f = jnp.where(crossing_out, mirrored, f)
    barrier = pltpu.get_barrier_semaphore()
    greeted = [(s, dev_next), (s, dev_prev), (s, dev_x), (s, dev_sib), before]
    greeted.append((SECTIONS - 1, mirrored))
    for device in greeted:
        pl.semaphore_signal(barrier, inc=1, device_id=device, device_id_type=MESH)
    pl.semaphore_wait(barrier, 5 + jnp.where(s == SECTIONS - 1, SECTIONS, 0))

    gather_a(0)
    gather_a(1)
    gather_b(0)
    gather_b(1)
    gather_c(0)
    gather_a(2)
    gather_c(1)
    gather_a(3)
    gather_d(0)
    gather_d(1)

    def hop(k, j):
        last = s == SECTIONS - 1
        second = k >= MICRO
        to_section = jnp.where(last, jnp.where(second, k - MICRO, 0), s + 1)
        slot = jnp.where(last, jnp.where(second, FINAL, k + MICRO), k)
        return pltpu.make_async_remote_copy(
            src_ref=outbox.at[k, j],
            dst_ref=inbox.at[slot, j],
            send_sem=hsend.at[k, j],
            recv_sem=hrecv.at[slot, j],
            device_id=(to_section, after_f),
            device_id_type=MESH,
        )

    def hop_arrived(slot, j):
        pltpu.make_async_remote_copy(
            src_ref=inbox.at[slot, j],
            dst_ref=inbox.at[slot, j],
            send_sem=hsend.at[0, j],
            recv_sem=hrecv.at[slot, j],
            device_id=(s, dev_sib),
            device_id_type=MESH,
        ).wait_recv()

    def layer(k):
        c = lax.div(k, MICRO)
        squares = jnp.zeros((LEN, 128), jnp.float32)
        for j in range(CHUNKS):
            hop_arrived(k, j)
            wide = inbox[k, j].astype(jnp.float32)
            for p in range(CW // 128):
                part = wide[:, p * 128 : (p + 1) * 128]
                squares = squares + part * part
            scaled = (wide * gain_ref[c, :, j * CW : (j + 1) * CW]).astype(jnp.bfloat16)
            for n in range(QKV // 512):
                cols = slice(n * 512, (n + 1) * 512)
                product = jnp.dot(
                    scaled,
                    wq[c, j * CW : (j + 1) * CW, cols],
                    preferred_element_type=jnp.float32,
                )
                if j > 0:
                    product = product + acc[:, cols]
                acc[:, cols] = product
        inv = lax.rsqrt(jnp.sum(squares, axis=1, keepdims=True) * (1.0 / D) + EPS)

        def projected(col, width=HEAD_DIM):
            cols = slice(col, col + width)
            return acc[:, cols] * inv + bias_ref[c, :, cols]

        def rotated(value, table):
            turned = pltpu.roll(value, HEAD_DIM // 2, 1)
            return value * rope_ref[table] + turned * rope_ref[table + 1]

        for g in range(KV_HEADS):
            key_high, key_low = split_two(rotated(projected(D + g * HEAD_DIM), 2))
            value_rows = projected(D + (KV_HEADS + g) * HEAD_DIM).astype(jnp.bfloat16)
            heads = [
                split_two(rotated(projected((g * GROUP + h) * HEAD_DIM), 0))
                for h in range(GROUP)
            ]
            query_high = jnp.concatenate([h[0] for h in heads], axis=0)
            query_low = jnp.concatenate([h[1] for h in heads], axis=0)
            contract = (((1,), (1,)), ((), ()))
            scores = lax.dot_general(
                jnp.concatenate([query_high, query_low, query_high], axis=1),
                jnp.concatenate([key_high, key_high, key_low], axis=1),
                contract,
                preferred_element_type=jnp.float32,
            )
            scores = scores + jnp.concatenate([mask_ref[...]] * GROUP, axis=0)
            weights = jnp.exp(scores - jnp.max(scores, axis=1, keepdims=True))
            paired = jnp.concatenate([value_rows, jnp.ones_like(value_rows)], axis=1)
            mixed = jnp.dot(
                weights.astype(jnp.bfloat16), paired, preferred_element_type=jnp.float32
            )
            context = (mixed[:, :HEAD_DIM] / mixed[:, HEAD_DIM:]).astype(jnp.bfloat16)
            for h in range(GROUP):
                col = (g * GROUP + h) * HEAD_DIM
                ctx[:, col : col + HEAD_DIM] = context[h * LEN : (h + 1) * LEN]

        for j in range(CHUNKS):
            update = jnp.dot(
                ctx[...],
                wo[c, :, j * CW : (j + 1) * CW],
                preferred_element_type=jnp.float32,
            )
            outbox[k, j] = (inbox[k, j].astype(jnp.float32) + update).astype(jnp.bfloat16)
            hop(k, j).start()

    def step(k, carry):
        layer(k)

        @pl.when(k == 2)
        def _():
            gather_b(2)

        @pl.when(k == 3)
        def _():
            gather_b(3)

        @pl.when(k == 5)
        def _():
            gather_c(2)

        @pl.when(k == 6)
        def _():
            gather_c(3)

        @pl.when(k == 7)
        def _():
            gather_d(2)
            gather_d(3)

        return carry

    lax.fori_loop(0, STEPS, step, 0)

    for j in range(CHUNKS):
        hop_arrived(FINAL, j)
        result_ref[:, j * CW : (j + 1) * CW] = inbox[FINAL, j]

    def drain(k, carry):
        for j in range(CHUNKS):
            hop(k, j).wait_send()
        return carry

    lax.fori_loop(0, STEPS, drain, 0)
    for t in range(4):
        for e in range(EVENTS):
            outgoing(t, e).wait_send()


def per_device(hidden_in, norm_gain, qkv_weight, qkv_bias, out_weight):
    rope, mask = tables()
    vmem = pl.BlockSpec(memory_space=pltpu.VMEM)
    anywhere = pl.BlockSpec(memory_space=pl.ANY)
    dma = pltpu.SemaphoreType.DMA
    result = pl.pallas_call(
        kernel,
        name="sections",
        out_shape=jax.ShapeDtypeStruct((LEN, D), jnp.bfloat16),
        in_specs=[anywhere, vmem, anywhere, vmem, anywhere, vmem, vmem],
        out_specs=vmem,
        scratch_shapes=[
            pltpu.VMEM((2, D, QKV), jnp.bfloat16),
            pltpu.VMEM((2, D, D), jnp.bfloat16),
            pltpu.VMEM((STEPS + 1, CHUNKS, LEN, CW), jnp.bfloat16),
            pltpu.VMEM((STEPS, CHUNKS, LEN, CW), jnp.bfloat16),
            pltpu.VMEM((LEN, QKV), jnp.float32),
            pltpu.VMEM((LEN, D), jnp.bfloat16),
            dma((4,)),
            dma((4, EVENTS)),
            dma((4, EVENTS)),
            dma((STEPS, CHUNKS)),
            dma((STEPS + 1, CHUNKS)),
        ],
        compiler_params=pltpu.CompilerParams(collective_id=0, has_side_effects=True),
    )(hidden_in, norm_gain, qkv_weight, qkv_bias, out_weight, rope, mask)
    return result[None, None]


def solution(mesh):
    in_specs = (
        P(None, "fsdp", None, None),
        P(None, "section", None),
        P(None, "section", "fsdp", None),
        P(None, "section", None),
        P(None, "section", "fsdp", None),
    )
    out_specs = P("section", "fsdp", None, None)
    return jax.shard_map(
        per_device, mesh=mesh, in_specs=in_specs, out_specs=out_specs, check_vma=False
    )
```

time: 737 us -> 209 us (0.28)
  waiting for transfers between devices: 269 us -> 0 us
  Pallas kernels: 0 us -> 207 us
  starting transfers between devices: 168 us -> 0 us
  matrix products: 143 us -> 0 us
  other arithmetic: 73.9 us -> 0 us
  local copies, waits for them, and re-layouts: 60.4 us -> 1.62 us
  between operations: 13.1 us -> 0.01 us
    pallas_call x0 -> x1, Pallas kernels: none -> 207 us  [per_device(): pl.pallas_call(kernel, name='sections', out_shape=jax.ShapeDtypeStruct((L...]
    ppermute x23 -> x0, starting transfers between devices: 168 us -> none  [passed_along(): return lax.ppermute(block, axis, route)]
    dot_general x64 -> x0, matrix products: 143 us -> none  [the longest x16 64.7 us: attend_layer(): jnp.dot(normed.reshape(rows * length, width), w_qkv, preferred_element_ty...]
    all_gather x2 -> x0, waiting for transfers between devices: 124 us -> none  [the longest x1 66.5 us: per_device(): lax.all_gather(qkv_weight[:, 0], 'fsdp', axis=1, tiled=True)]
    psum x1 -> x0, waiting for transfers between devices: 88.6 us -> none  [from_root(): return lax.psum(kept, axis)]
    ppermute x23 -> x0, waiting for transfers between devices: 54.7 us -> none  [passed_along(): return lax.ppermute(block, axis, route)]
    dynamic_update_slice x46 -> x0, other arithmetic: 33.9 us -> none  [the longest x23 17.1 us: advance(): lax.dynamic_update_index_in_dim(result, jnp.where(owned, block_out, previ...]
    dynamic_slice x23 -> x0, other arithmetic: 26.4 us -> none  [advance(): before = lax.dynamic_index_in_dim(waiting, got_slot, 0, keepdims=False)]
  transfers between devices with their start and end apart: 26 -> 0, of which waited for: 26 -> 0; matrix products, arithmetic and copies ran while one was open for 7% -> 0% of each run, Pallas kernels for 0% -> 0%
where the time goes in v1:
time: 209 us
  Pallas kernels  207 us (99%)
    pallas_call x1, Pallas kernels, per_device(): pl.pallas_call(kernel, name='sections', out_shape=jax.ShapeDtypeStruct((L...  207 us

profile of v1, /device:TPU:100, one launch (start us, length us, event | category | flops | bytes accessed | tf_op | source)
XLA Modules:
  0.0 208.6 jit_solution(14291278615685304610)
XLA Ops:
  0.0 207.0 %sections.1 = bf16[64,1536]{1,0:T(8,128)(2,1)} custom-call(bf16[8,1,64,1536]{3,2,1,0:T(8,128)(2,1)} %hidden_hbm.1, f32[2,1,1536]{2,1,0:T(1,128)} %gain_ref.1, bf16[2,1,96,2048]{3,2,1,0:T(8,128)(2,1)} %qkv_hbm.1, f32[2,1,2048]{2,1,0:T(1,128)} %bias_ref.1, bf16[2,1,96,1536]{3,2,1,0:T(8,128)(2,1)} %out_hbm.1, f32[4,64,128]{2,1,0:T(8,128)} %constant.4.clone.rope_ref, ...), custom_call_target="tpu_custom_call" | custom-call | tf_op jit(solution)/shard_map/sections/pallas_call | solution.py:364
  207.0 1.6 copy.9

commit v2 on v1

--- a/solution.py
+++ b/solution.py
@@ -14,6 +14,8 @@
 HEAD_DIM = 128
 GROUP = HEADS // KV_HEADS
 LEN = 64
+PIECE = 32
+PIECES = LEN // PIECE
 D = HEADS * HEAD_DIM
 QKV = D + 2 * KV_HEADS * HEAD_DIM
 SECTIONS = 8
@@ -21,13 +23,15 @@
 ROWS = D // FSDP
 HALF = ROWS // 2
 MICRO = 8
-STEPS = 2 * MICRO
+PASS = MICRO * PIECES
+STEPS = 2 * PASS
 CHUNKS = 3
 CW = D // CHUNKS
 FINAL = STEPS
 THETA = 1000000.0
 EPS = 1.0
-EVENTS = 16
+EVENTS = 18
+SLAB = 80
 MESH = pl.DeviceIdType.MESH
 
 
@@ -40,6 +44,8 @@
     scale = 1.0 / math.sqrt(HEAD_DIM)
     mask = np.where(np.arange(LEN)[:, None] >= np.arange(LEN)[None, :], 0.0, -1e30)
     rope = np.stack([full_cos * scale, full_sin * scale, full_cos, full_sin])
+    rope = rope.reshape(4, PIECES, PIECE, HEAD_DIM).swapaxes(0, 1)
+    mask = mask.reshape(PIECES, PIECE, LEN)
     return rope.astype(np.float32), mask.astype(np.float32)
 
 
@@ -64,6 +70,8 @@
     outbox,
     acc,
     ctx,
+    keys,
+    values,
     own_sem,
     gsend,
     grecv,
@@ -114,9 +122,11 @@
         2: (OWN, 0, ROWS, dev_x),
         3: (PREV, 0, HALF, dev_next),
         4: (NEXT, HALF, HALF, dev_prev),
-        5: (ACROSS, 0, ROWS, dev_next),
-        6: (ACROSS, 0, ROWS, dev_prev),
+        5: (ACROSS, 0, SLAB, dev_next),
+        6: (ACROSS, 0, SLAB, dev_prev),
         7: (FAR, 0, ROWS, dev_x),
+        16: (PREV, SLAB, ROWS - SLAB, dev_x),
+        17: (NEXT, SLAB, ROWS - SLAB, dev_x),
     }
     lands = {
         0: (PREV, 0, ROWS),
@@ -124,9 +134,11 @@
         2: (ACROSS, 0, ROWS),
         3: (FAR, 0, HALF),
         4: (FAR, HALF, HALF),
-        5: (XPREV, 0, ROWS),
-        6: (XNEXT, 0, ROWS),
+        5: (XPREV, 0, SLAB),
+        6: (XNEXT, 0, SLAB),
         7: (XFAR, 0, ROWS),
+        16: (XPREV, SLAB, ROWS - SLAB),
+        17: (XNEXT, SLAB, ROWS - SLAB),
     }
     for n in range(8):
         sends[8 + n] = (blocks[n], 0, ROWS, dev_sib)
@@ -166,30 +178,37 @@
             outgoing(t, e).start()
 
     def gather_b(t):
-        for e, then in ((0, (3, 9)), (1, (4, 10)), (2, (5, 6, 11))):
+        for e, then in ((0, (3, 16, 9)), (1, (4, 17, 10))):
             arrived(t, e)
             for n in then:
                 outgoing(t, n).start()
 
     def gather_c(t):
+        arrived(t, 2)
+        for n in (5, 6, 11):
+            outgoing(t, n).start()
+
+    def gather_d(t):
         arrived(t, 3)
         arrived(t, 4)
         for n in (7, 12):
             outgoing(t, n).start()
-        arrived(t, 5)
-        outgoing(t, 13).start()
-        arrived(t, 6)
-        outgoing(t, 14).start()
-
-    def gather_d(t):
-        arrived(t, 7)
-        outgoing(t, 15).start()
+
+    def gather_e(t):
+        for e, then in ((5, None), (16, 13), (6, None), (17, 14), (7, 15)):
+            arrived(t, e)
+            if then is not None:
+                outgoing(t, then).start()
+
+    def gather_f(t):
         for e in range(8, 16):
             arrived(t, e)
 
     def entering(k, j):
         return pltpu.make_async_copy(
-            hidden_hbm.at[k, 0, :, pl.ds(j * CW, CW)], inbox.at[k, j], hrecv.at[k, j]
+            hidden_hbm.at[k // PIECES, 0, pl.ds(k % PIECES * PIECE, PIECE), pl.ds(j * CW, CW)],
+            inbox.at[k, j],
+            hrecv.at[k, j],
         )
 
     for t in range(4):
@@ -197,7 +216,7 @@
 
     @pl.when(s == 0)
     def _():
-        for k in range(MICRO):
+        for k in range(PASS):
             for j in range(CHUNKS):
                 entering(k, j).start()
 
@@ -214,20 +233,33 @@
 
     gather_a(0)
     gather_a(1)
+    keys[...] = jnp.zeros_like(keys)
+    values[...] = jnp.ones_like(values)
     gather_b(0)
     gather_b(1)
     gather_c(0)
-    gather_a(2)
     gather_c(1)
-    gather_a(3)
     gather_d(0)
     gather_d(1)
+    gather_e(0)
+    gather_f(0)
+
+    def settle():
+        gather_e(1)
+        gather_f(1)
+        gather_a(2)
+        gather_a(3)
+
+    @pl.when(s > 0)
+    def _():
+        settle()
 
     def hop(k, j):
         last = s == SECTIONS - 1
-        second = k >= MICRO
-        to_section = jnp.where(last, jnp.where(second, k - MICRO, 0), s + 1)
-        slot = jnp.where(last, jnp.where(second, FINAL, k + MICRO), k)
+        second = k >= PASS
+        owner = lax.div(k, PIECES) - MICRO
+        to_section = jnp.where(last, jnp.where(second, owner, 0), s + 1)
+        slot = jnp.where(last, jnp.where(second, FINAL + lax.rem(k, PIECES), k + PASS), k)
         return pltpu.make_async_remote_copy(
             src_ref=outbox.at[k, j],
             dst_ref=inbox.at[slot, j],
@@ -248,8 +280,9 @@
         ).wait_recv()
 
     def layer(k):
-        c = lax.div(k, MICRO)
-        squares = jnp.zeros((LEN, 128), jnp.float32)
+        c = lax.div(k, PASS)
+        piece = lax.rem(k, PIECES)
+        squares = jnp.zeros((PIECE, 128), jnp.float32)
         for j in range(CHUNKS):
             hop_arrived(k, j)
             wide = inbox[k, j].astype(jnp.float32)
@@ -275,17 +308,24 @@
 
         def rotated(value, table):
             turned = pltpu.roll(value, HEAD_DIM // 2, 1)
-            return value * rope_ref[table] + turned * rope_ref[table + 1]
-
+            return value * rope_ref[piece, table] + turned * rope_ref[piece, table + 1]
+
+        rows = pl.ds(pl.multiple_of(piece * PIECE, PIECE), PIECE)
         for g in range(KV_HEADS):
             key_high, key_low = split_two(rotated(projected(D + g * HEAD_DIM), 2))
-            value_rows = projected(D + (KV_HEADS + g) * HEAD_DIM).astype(jnp.bfloat16)
+            keys[g, rows, :HEAD_DIM] = key_high
+            keys[g, rows, HEAD_DIM:] = key_low
+            value_rows = projected(D + (KV_HEADS + g) * HEAD_DIM)
+            values[g, rows, :HEAD_DIM] = value_rows.astype(jnp.bfloat16)
+        for g in range(KV_HEADS):
             heads = [
                 split_two(rotated(projected((g * GROUP + h) * HEAD_DIM), 0))
                 for h in range(GROUP)
             ]
             query_high = jnp.concatenate([h[0] for h in heads], axis=0)
             query_low = jnp.concatenate([h[1] for h in heads], axis=0)
+            key_high = keys[g, :, :HEAD_DIM]
+            key_low = keys[g, :, HEAD_DIM:]
             contract = (((1,), (1,)), ((), ()))
             scores = lax.dot_general(
                 jnp.concatenate([query_high, query_low, query_high], axis=1),
@@ -293,16 +333,19 @@
                 contract,
                 preferred_element_type=jnp.float32,
             )
-            scores = scores + jnp.concatenate([mask_ref[...]] * GROUP, axis=0)
+            scores = scores + jnp.concatenate([mask_ref[piece]] * GROUP, axis=0)
             weights = jnp.exp(scores - jnp.max(scores, axis=1, keepdims=True))
-            paired = jnp.concatenate([value_rows, jnp.ones_like(value_rows)], axis=1)
             mixed = jnp.dot(
-                weights.astype(jnp.bfloat16), paired, preferred_element_type=jnp.float32
+                weights.astype(jnp.bfloat16), values[g], preferred_element_type=jnp.float32
             )
             context = (mixed[:, :HEAD_DIM] / mixed[:, HEAD_DIM:]).astype(jnp.bfloat16)
             for h in range(GROUP):
                 col = (g * GROUP + h) * HEAD_DIM
-                ctx[:, col : col + HEAD_DIM] = context[h * LEN : (h + 1) * LEN]
+                ctx[:, col : col + HEAD_DIM] = context[h * PIECE : (h + 1) * PIECE]
+
+        @pl.when((k == 0) & (s == 0))
+        def _():
+            settle()
 
         for j in range(CHUNKS):
             update = jnp.dot(
@@ -316,34 +359,35 @@
     def step(k, carry):
         layer(k)
 
-        @pl.when(k == 2)
+        @pl.when(k == 4)
         def _():
             gather_b(2)
 
-        @pl.when(k == 3)
+        @pl.when(k == 7)
         def _():
             gather_b(3)
-
-        @pl.when(k == 5)
-        def _():
             gather_c(2)
-
-        @pl.when(k == 6)
-        def _():
             gather_c(3)
 
-        @pl.when(k == 7)
+        @pl.when(k == 9)
         def _():
             gather_d(2)
             gather_d(3)
 
+        @pl.when(k == 15)
+        def _():
+            for t in (2, 3):
+                gather_e(t)
+                gather_f(t)
+
         return carry
 
     lax.fori_loop(0, STEPS, step, 0)
 
-    for j in range(CHUNKS):
-        hop_arrived(FINAL, j)
-        result_ref[:, j * CW : (j + 1) * CW] = inbox[FINAL, j]
+    for n in range(PIECES):
+        for j in range(CHUNKS):
+            hop_arrived(FINAL + n, j)
+            result_ref[n * PIECE : (n + 1) * PIECE, j * CW : (j + 1) * CW] = inbox[FINAL + n, j]
 
     def drain(k, carry):
         for j in range(CHUNKS):
@@ -370,15 +414,17 @@
         scratch_shapes=[
             pltpu.VMEM((2, D, QKV), jnp.bfloat16),
             pltpu.VMEM((2, D, D), jnp.bfloat16),
-            pltpu.VMEM((STEPS + 1, CHUNKS, LEN, CW), jnp.bfloat16),
-            pltpu.VMEM((STEPS, CHUNKS, LEN, CW), jnp.bfloat16),
-            pltpu.VMEM((LEN, QKV), jnp.float32),
-            pltpu.VMEM((LEN, D), jnp.bfloat16),
+            pltpu.VMEM((STEPS + PIECES, CHUNKS, PIECE, CW), jnp.bfloat16),
+            pltpu.VMEM((STEPS, CHUNKS, PIECE, CW), jnp.bfloat16),
+            pltpu.VMEM((PIECE, QKV), jnp.float32),
+            pltpu.VMEM((PIECE, D), jnp.bfloat16),
+            pltpu.VMEM((KV_HEADS, LEN, 2 * HEAD_DIM), jnp.bfloat16),
+            pltpu.VMEM((KV_HEADS, LEN, 2 * HEAD_DIM), jnp.bfloat16),
             dma((4,)),
             dma((4, EVENTS)),
             dma((4, EVENTS)),
             dma((STEPS, CHUNKS)),
-            dma((STEPS + 1, CHUNKS)),
+            dma((STEPS + PIECES, CHUNKS)),
         ],
         compiler_params=pltpu.CompilerParams(collective_id=0, has_side_effects=True),
     )(hidden_in, norm_gain, qkv_weight, qkv_bias, out_weight, rope, mask)

time: 209 us -> 194 us (0.928)
  Pallas kernels: 207 us -> 192 us
    pallas_call x1, Pallas kernels: 207 us -> 192 us  [per_device(): pl.pallas_call(kernel, name='sections', out_shape=jax.ShapeDtypeStruct((L...]
where the time goes in v2:
time: 194 us
  Pallas kernels  192 us (99%)
    pallas_call x1, Pallas kernels, per_device(): pl.pallas_call(kernel, name='sections', out_shape=jax.ShapeDtypeStruct((L...  192 us

profile of v2, /device:TPU:100, one launch (start us, length us, event | category | flops | bytes accessed | tf_op | source)
XLA Modules:
  0.0 193.8 jit_solution(13481797312391779432)
XLA Ops:
  0.0 192.1 %sections.1 = bf16[64,1536]{1,0:T(8,128)(2,1)} custom-call(bf16[8,1,64,1536]{3,2,1,0:T(8,128)(2,1)} %hidden_hbm.1, f32[2,1,1536]{2,1,0:T(1,128)} %gain_ref.1, bf16[2,1,96,2048]{3,2,1,0:T(8,128)(2,1)} %qkv_hbm.1, f32[2,1,2048]{2,1,0:T(1,128)} %bias_ref.1, bf16[2,1,96,1536]{3,2,1,0:T(8,128)(2,1)} %out_hbm.1, f32[2,4,32,128]{3,2,1,0:T(8,128)} %constant.4.clone.rope_ref, ...), custom_call_target="tpu_custom_call" | custom-call | tf_op jit(solution)/shard_map/sections/pallas_call | solution.py:408
  192.2 1.6 copy.9

commit v3 on v2

--- a/solution.py
+++ b/solution.py
@@ -69,7 +69,6 @@
     inbox,
     outbox,
     acc,
-    ctx,
     keys,
     values,
     own_sem,
@@ -244,15 +243,10 @@
     gather_e(0)
     gather_f(0)
 
-    def settle():
-        gather_e(1)
-        gather_f(1)
-        gather_a(2)
-        gather_a(3)
-
-    @pl.when(s > 0)
-    def _():
-        settle()
+    gather_e(1)
+    gather_f(1)
+    gather_a(2)
+    gather_a(3)
 
     def hop(k, j):
         last = s == SECTIONS - 1
@@ -290,7 +284,7 @@
                 part = wide[:, p * 128 : (p + 1) * 128]
                 squares = squares + part * part
             scaled = (wide * gain_ref[c, :, j * CW : (j + 1) * CW]).astype(jnp.bfloat16)
-            for n in range(QKV // 512):
+            for n in (3, 0, 1, 2):
                 cols = slice(n * 512, (n + 1) * 512)
                 product = jnp.dot(
                     scaled,
@@ -317,6 +311,8 @@
             keys[g, rows, HEAD_DIM:] = key_low
             value_rows = projected(D + (KV_HEADS + g) * HEAD_DIM)
             values[g, rows, :HEAD_DIM] = value_rows.astype(jnp.bfloat16)
+        half = GROUP * HEAD_DIM
+        updates = [None] * CHUNKS
         for g in range(KV_HEADS):
             heads = [
                 split_two(rotated(projected((g * GROUP + h) * HEAD_DIM), 0))
@@ -339,22 +335,25 @@
                 weights.astype(jnp.bfloat16), values[g], preferred_element_type=jnp.float32
             )
             context = (mixed[:, :HEAD_DIM] / mixed[:, HEAD_DIM:]).astype(jnp.bfloat16)
-            for h in range(GROUP):
-                col = (g * GROUP + h) * HEAD_DIM
-                ctx[:, col : col + HEAD_DIM] = context[h * PIECE : (h + 1) * PIECE]
-
-        @pl.when((k == 0) & (s == 0))
-        def _():
-            settle()
-
-        for j in range(CHUNKS):
-            update = jnp.dot(
-                ctx[...],
-                wo[c, :, j * CW : (j + 1) * CW],
-                preferred_element_type=jnp.float32,
+            context = jnp.concatenate(
+                [context[h * PIECE : (h + 1) * PIECE] for h in range(GROUP)], axis=1
             )
-            outbox[k, j] = (inbox[k, j].astype(jnp.float32) + update).astype(jnp.bfloat16)
-            hop(k, j).start()
+
+            def finish(j):
+                total = inbox[k, j].astype(jnp.float32) + updates[j]
+                outbox[k, j] = total.astype(jnp.bfloat16)
+                hop(k, j).start()
+
+            for j in range(CHUNKS):
+                product = jnp.dot(
+                    context,
+                    wo[c, g * half : (g + 1) * half, j * CW : (j + 1) * CW],
+                    preferred_element_type=jnp.float32,
+                )
+                updates[j] = product if g == 0 else updates[j] + product
+                if g > 0 and j > 0:
+                    finish(j - 1)
+        finish(CHUNKS - 1)
 
     def step(k, carry):
         layer(k)
@@ -417,7 +416,6 @@
             pltpu.VMEM((STEPS + PIECES, CHUNKS, PIECE, CW), jnp.bfloat16),
             pltpu.VMEM((STEPS, CHUNKS, PIECE, CW), jnp.bfloat16),
             pltpu.VMEM((PIECE, QKV), jnp.float32),
-            pltpu.VMEM((PIECE, D), jnp.bfloat16),
             pltpu.VMEM((KV_HEADS, LEN, 2 * HEAD_DIM), jnp.bfloat16),
             pltpu.VMEM((KV_HEADS, LEN, 2 * HEAD_DIM), jnp.bfloat16),
             dma((4,)),

time: 194 us -> 185 us (0.954)
  Pallas kernels: 192 us -> 183 us
    pallas_call x1, Pallas kernels: 192 us -> 183 us  [per_device(): pl.pallas_call(kernel, name='sections', out_shape=jax.ShapeDtypeStruct((L...]
where the time goes in v3:
time: 185 us
  Pallas kernels  183 us (99%)
    pallas_call x1, Pallas kernels, per_device(): pl.pallas_call(kernel, name='sections', out_shape=jax.ShapeDtypeStruct((L...  183 us

profile of v3, /device:TPU:100, one launch (start us, length us, event | category | flops | bytes accessed | tf_op | source)
XLA Modules:
  0.0 184.5 jit_solution(8883219019817524087)
XLA Ops:
  0.0 182.9 %sections.1 = bf16[64,1536]{1,0:T(8,128)(2,1)} custom-call(bf16[8,1,64,1536]{3,2,1,0:T(8,128)(2,1)} %hidden_hbm.1, f32[2,1,1536]{2,1,0:T(1,128)} %gain_ref.1, bf16[2,1,96,2048]{3,2,1,0:T(8,128)(2,1)} %qkv_hbm.1, f32[2,1,2048]{2,1,0:T(1,128)} %bias_ref.1, bf16[2,1,96,1536]{3,2,1,0:T(8,128)(2,1)} %out_hbm.1, f32[2,4,32,128]{3,2,1,0:T(8,128)} %constant.4.clone.rope_ref, ...), custom_call_target="tpu_custom_call" | custom-call | tf_op jit(solution)/shard_map/sections/pallas_call | solution.py:407
  182.9 1.6 copy.9

commit v4 on v3

--- a/solution.py
+++ b/solution.py
@@ -311,8 +311,9 @@
             keys[g, rows, HEAD_DIM:] = key_low
             value_rows = projected(D + (KV_HEADS + g) * HEAD_DIM)
             values[g, rows, :HEAD_DIM] = value_rows.astype(jnp.bfloat16)
-        half = GROUP * HEAD_DIM
-        updates = [None] * CHUNKS
+        contract = (((1,), (1,)), ((), ()))
+        mask = jnp.concatenate([mask_ref[piece]] * GROUP, axis=0)
+        scores = []
         for g in range(KV_HEADS):
             heads = [
                 split_two(rotated(projected((g * GROUP + h) * HEAD_DIM), 0))
@@ -322,37 +323,50 @@
             query_low = jnp.concatenate([h[1] for h in heads], axis=0)
             key_high = keys[g, :, :HEAD_DIM]
             key_low = keys[g, :, HEAD_DIM:]
-            contract = (((1,), (1,)), ((), ()))
-            scores = lax.dot_general(
-                jnp.concatenate([query_high, query_low, query_high], axis=1),
-                jnp.concatenate([key_high, key_high, key_low], axis=1),
-                contract,
-                preferred_element_type=jnp.float32,
+            scores.append(
+                lax.dot_general(
+                    jnp.concatenate([query_high, query_low, query_high], axis=1),
+                    jnp.concatenate([key_high, key_high, key_low], axis=1),
+                    contract,
+                    preferred_element_type=jnp.float32,
+                )
             )
-            scores = scores + jnp.concatenate([mask_ref[piece]] * GROUP, axis=0)
-            weights = jnp.exp(scores - jnp.max(scores, axis=1, keepdims=True))
-            mixed = jnp.dot(
-                weights.astype(jnp.bfloat16), values[g], preferred_element_type=jnp.float32
+        weights = []
+        for g in range(KV_HEADS):
+            masked = scores[g] + mask
+            shifted = masked - jnp.max(masked, axis=1, keepdims=True)
+            weights.append(jnp.exp(shifted).astype(jnp.bfloat16))
+        mixed = [
+            jnp.dot(weights[g], values[g], preferred_element_type=jnp.float32)
+            for g in range(KV_HEADS)
+        ]
+        contexts = []
+        for g in range(KV_HEADS):
+            context = (mixed[g][:, :HEAD_DIM] / mixed[g][:, HEAD_DIM:]).astype(jnp.bfloat16)
+            contexts.append(
+                jnp.concatenate(
+                    [context[h * PIECE : (h + 1) * PIECE] for h in range(GROUP)], axis=1
+                )
             )
-            context = (mixed[:, :HEAD_DIM] / mixed[:, HEAD_DIM:]).astype(jnp.bfloat16)
-            context = jnp.concatenate(
-                [context[h * PIECE : (h + 1) * PIECE] for h in range(GROUP)], axis=1
-            )
-
-            def finish(j):
-                total = inbox[k, j].astype(jnp.float32) + updates[j]
-                outbox[k, j] = total.astype(jnp.bfloat16)
-                hop(k, j).start()
-
-            for j in range(CHUNKS):
+
+        updates = [None] * CHUNKS
+        half = GROUP * HEAD_DIM
+
+        def finish(j):
+            total = inbox[k, j].astype(jnp.float32) + updates[j]
+            outbox[k, j] = total.astype(jnp.bfloat16)
+            hop(k, j).start()
+
+        for j in range(CHUNKS):
+            for g in range(KV_HEADS):
                 product = jnp.dot(
-                    context,
+                    contexts[g],
                     wo[c, g * half : (g + 1) * half, j * CW : (j + 1) * CW],
                     preferred_element_type=jnp.float32,
                 )
                 updates[j] = product if g == 0 else updates[j] + product
-                if g > 0 and j > 0:
-                    finish(j - 1)
+            if j > 0:
+                finish(j - 1)
         finish(CHUNKS - 1)
 
     def step(k, carry):

time: 185 us -> 174 us (0.941)
  Pallas kernels: 183 us -> 173 us
    pallas_call x1, Pallas kernels: 183 us -> 173 us  [per_device(): pl.pallas_call(kernel, name='sections', out_shape=jax.ShapeDtypeStruct((L...]
where the time goes in v4:
time: 174 us
  Pallas kernels  173 us (99%)
    pallas_call x1, Pallas kernels, per_device(): pl.pallas_call(kernel, name='sections', out_shape=jax.ShapeDtypeStruct((L...  173 us

profile of v4, /device:TPU:100, one launch (start us, length us, event | category | flops | bytes accessed | tf_op | source)
XLA Modules:
  0.0 174.3 jit_solution(8594477540970422246)
XLA Ops:
  0.0 172.6 %sections.1 = bf16[64,1536]{1,0:T(8,128)(2,1)} custom-call(bf16[8,1,64,1536]{3,2,1,0:T(8,128)(2,1)} %hidden_hbm.1, f32[2,1,1536]{2,1,0:T(1,128)} %gain_ref.1, bf16[2,1,96,2048]{3,2,1,0:T(8,128)(2,1)} %qkv_hbm.1, f32[2,1,2048]{2,1,0:T(1,128)} %bias_ref.1, bf16[2,1,96,1536]{3,2,1,0:T(8,128)(2,1)} %out_hbm.1, f32[2,4,32,128]{3,2,1,0:T(8,128)} %constant.4.clone.rope_ref, ...), custom_call_target="tpu_custom_call" | custom-call | tf_op jit(solution)/shard_map/sections/pallas_call | solution.py:421
  172.6 1.6 copy.9

commit v5 on v4

--- a/solution.py
+++ b/solution.py
@@ -30,7 +30,6 @@
 FINAL = STEPS
 THETA = 1000000.0
 EPS = 1.0
-EVENTS = 18
 SLAB = 80
 MESH = pl.DeviceIdType.MESH
 
@@ -143,14 +142,17 @@
         sends[8 + n] = (blocks[n], 0, ROWS, dev_sib)
         lands[8 + n] = (blocks[n] + flip, 0, ROWS)
 
+    def arrival(e):
+        return e if e < 8 else 8 if e < 16 else e - 7
+
     def outgoing(t, e):
         block, first, count, target = sends[e]
         part = region(t, block, first, count)
         return pltpu.make_async_remote_copy(
             src_ref=part,
             dst_ref=part,
-            send_sem=gsend.at[t, e],
-            recv_sem=grecv.at[t, e],
+            send_sem=gsend.at[t],
+            recv_sem=grecv.at[t, arrival(e)],
             device_id=(s, target),
             device_id_type=MESH,
         )
@@ -161,8 +163,8 @@
         pltpu.make_async_remote_copy(
             src_ref=part,
             dst_ref=part,
-            send_sem=gsend.at[t, e],
-            recv_sem=grecv.at[t, e],
+            send_sem=gsend.at[t],
+            recv_sem=grecv.at[t, arrival(e)],
             device_id=(s, dev_sib),
             device_id_type=MESH,
         ).wait_recv()
@@ -200,8 +202,26 @@
                 outgoing(t, then).start()
 
     def gather_f(t):
-        for e in range(8, 16):
-            arrived(t, e)
+        whole = region(t, 0, 0, 8 * ROWS)
+        pltpu.make_async_remote_copy(
+            src_ref=whole,
+            dst_ref=whole,
+            send_sem=gsend.at[t],
+            recv_sem=grecv.at[t, 8],
+            device_id=(s, dev_sib),
+            device_id_type=MESH,
+        ).wait_recv()
+
+    def gather_sent(t):
+        whole = region(t, 0, 0, sum(count for _, _, count, _ in sends.values()))
+        pltpu.make_async_remote_copy(
+            src_ref=whole,
+            dst_ref=whole,
+            send_sem=gsend.at[t],
+            recv_sem=grecv.at[t, 8],
+            device_id=(s, dev_sib),
+            device_id_type=MESH,
+        ).wait_send()
 
     def entering(k, j):
         return pltpu.make_async_copy(
@@ -257,7 +277,7 @@
         return pltpu.make_async_remote_copy(
             src_ref=outbox.at[k, j],
             dst_ref=inbox.at[slot, j],
-            send_sem=hsend.at[k, j],
+            send_sem=hsend.at[0],
             recv_sem=hrecv.at[slot, j],
             device_id=(to_section, after_f),
             device_id_type=MESH,
@@ -267,7 +287,7 @@
         pltpu.make_async_remote_copy(
             src_ref=inbox.at[slot, j],
             dst_ref=inbox.at[slot, j],
-            send_sem=hsend.at[0, j],
+            send_sem=hsend.at[0],
             recv_sem=hrecv.at[slot, j],
             device_id=(s, dev_sib),
             device_id_type=MESH,
@@ -397,20 +417,21 @@
 
     lax.fori_loop(0, STEPS, step, 0)
 
+    pltpu.make_async_remote_copy(
+        src_ref=outbox,
+        dst_ref=outbox,
+        send_sem=hsend.at[0],
+        recv_sem=hrecv.at[0, 0],
+        device_id=(s, dev_sib),
+        device_id_type=MESH,
+    ).wait_send()
+    for t in range(4):
+        gather_sent(t)
+
     for n in range(PIECES):
         for j in range(CHUNKS):
             hop_arrived(FINAL + n, j)
             result_ref[n * PIECE : (n + 1) * PIECE, j * CW : (j + 1) * CW] = inbox[FINAL + n, j]
-
-    def drain(k, carry):
-        for j in range(CHUNKS):
-            hop(k, j).wait_send()
-        return carry
-
-    lax.fori_loop(0, STEPS, drain, 0)
-    for t in range(4):
-        for e in range(EVENTS):
-            outgoing(t, e).wait_send()
 
 
 def per_device(hidden_in, norm_gain, qkv_weight, qkv_bias, out_weight):
@@ -433,9 +454,9 @@
             pltpu.VMEM((KV_HEADS, LEN, 2 * HEAD_DIM), jnp.bfloat16),
             pltpu.VMEM((KV_HEADS, LEN, 2 * HEAD_DIM), jnp.bfloat16),
             dma((4,)),
-            dma((4, EVENTS)),
-            dma((4, EVENTS)),
-            dma((STEPS, CHUNKS)),
+            dma((4,)),
+            dma((4, 11)),
+            dma((1,)),
             dma((STEPS + PIECES, CHUNKS)),
         ],
         compiler_params=pltpu.CompilerParams(collective_id=0, has_side_effects=True),

time: 174 us -> 172 us (0.989)
  Pallas kernels: 173 us -> 170 us
    pallas_call x1, Pallas kernels: 173 us -> 170 us  [per_device(): pl.pallas_call(kernel, name='sections', out_shape=jax.ShapeDtypeStruct((L...]
where the time goes in v5:
time: 172 us
  Pallas kernels  170 us (99%)
    pallas_call x1, Pallas kernels, per_device(): pl.pallas_call(kernel, name='sections', out_shape=jax.ShapeDtypeStruct((L...  170 us

profile of v5, /device:TPU:100, one launch (start us, length us, event | category | flops | bytes accessed | tf_op | source)
XLA Modules:
  0.0 171.7 jit_solution(7625699692646099086)
XLA Ops:
  0.0 170.0 %sections.1 = bf16[64,1536]{1,0:T(8,128)(2,1)} custom-call(bf16[8,1,64,1536]{3,2,1,0:T(8,128)(2,1)} %hidden_hbm.1, f32[2,1,1536]{2,1,0:T(1,128)} %gain_ref.1, bf16[2,1,96,2048]{3,2,1,0:T(8,128)(2,1)} %qkv_hbm.1, f32[2,1,2048]{2,1,0:T(1,128)} %bias_ref.1, bf16[2,1,96,1536]{3,2,1,0:T(8,128)(2,1)} %out_hbm.1, f32[2,4,32,128]{3,2,1,0:T(8,128)} %constant.4.clone.rope_ref, ...), custom_call_target="tpu_custom_call" | custom-call | tf_op jit(solution)/shard_map/sections/pallas_call | solution.py:442
  170.0 1.6 copy.9

commit v6 on v5

--- a/solution.py
+++ b/solution.py
@@ -130,20 +130,17 @@
         0: (PREV, 0, ROWS),
         1: (NEXT, 0, ROWS),
         2: (ACROSS, 0, ROWS),
-        3: (FAR, 0, HALF),
-        4: (FAR, HALF, HALF),
-        5: (XPREV, 0, SLAB),
-        6: (XNEXT, 0, SLAB),
+        3: (FAR, 0, ROWS),
+        5: (XPREV, 0, ROWS),
+        6: (XNEXT, 0, ROWS),
         7: (XFAR, 0, ROWS),
-        16: (XPREV, SLAB, ROWS - SLAB),
-        17: (XNEXT, SLAB, ROWS - SLAB),
     }
     for n in range(8):
         sends[8 + n] = (blocks[n], 0, ROWS, dev_sib)
         lands[8 + n] = (blocks[n] + flip, 0, ROWS)
 
     def arrival(e):
-        return e if e < 8 else 8 if e < 16 else e - 7
+        return {4: 3, 5: 4, 16: 4, 6: 5, 17: 5, 7: 6}.get(e, e if e < 4 else 7)
 
     def outgoing(t, e):
         block, first, count, target = sends[e]
@@ -191,15 +188,13 @@
 
     def gather_d(t):
         arrived(t, 3)
-        arrived(t, 4)
         for n in (7, 12):
             outgoing(t, n).start()
 
     def gather_e(t):
-        for e, then in ((5, None), (16, 13), (6, None), (17, 14), (7, 15)):
+        for e, then in ((5, 13), (6, 14), (7, 15)):
             arrived(t, e)
-            if then is not None:
-                outgoing(t, then).start()
+            outgoing(t, then).start()
 
     def gather_f(t):
         whole = region(t, 0, 0, 8 * ROWS)
@@ -207,7 +202,7 @@
             src_ref=whole,
             dst_ref=whole,
             send_sem=gsend.at[t],
-            recv_sem=grecv.at[t, 8],
+            recv_sem=grecv.at[t, arrival(8)],
             device_id=(s, dev_sib),
             device_id_type=MESH,
         ).wait_recv()
@@ -218,16 +213,19 @@
             src_ref=whole,
             dst_ref=whole,
             send_sem=gsend.at[t],
-            recv_sem=grecv.at[t, 8],
+            recv_sem=grecv.at[t, arrival(8)],
             device_id=(s, dev_sib),
             device_id_type=MESH,
         ).wait_send()
+
+    def arrival_row(slot):
+        return slot % PASS
 
     def entering(k, j):
         return pltpu.make_async_copy(
             hidden_hbm.at[k // PIECES, 0, pl.ds(k % PIECES * PIECE, PIECE), pl.ds(j * CW, CW)],
             inbox.at[k, j],
-            hrecv.at[k, j],
+            hrecv.at[arrival_row(k), j],
         )
 
     for t in range(4):
@@ -274,11 +272,14 @@
         owner = lax.div(k, PIECES) - MICRO
         to_section = jnp.where(last, jnp.where(second, owner, 0), s + 1)
         slot = jnp.where(last, jnp.where(second, FINAL + lax.rem(k, PIECES), k + PASS), k)
+        done = last & second
+        row = jnp.where(done, PASS, lax.rem(k, PASS))
+        column = jnp.where(done, 0, j)
         return pltpu.make_async_remote_copy(
             src_ref=outbox.at[k, j],
             dst_ref=inbox.at[slot, j],
             send_sem=hsend.at[0],
-            recv_sem=hrecv.at[slot, j],
+            recv_sem=hrecv.at[row, column],
             device_id=(to_section, after_f),
             device_id_type=MESH,
         )
@@ -288,7 +289,7 @@
             src_ref=inbox.at[slot, j],
             dst_ref=inbox.at[slot, j],
             send_sem=hsend.at[0],
-            recv_sem=hrecv.at[slot, j],
+            recv_sem=hrecv.at[lax.rem(slot, PASS), j],
             device_id=(s, dev_sib),
             device_id_type=MESH,
         ).wait_recv()
@@ -428,9 +429,17 @@
     for t in range(4):
         gather_sent(t)
 
+    finished = inbox.at[pl.ds(FINAL, PIECES)]
+    pltpu.make_async_remote_copy(
+        src_ref=finished,
+        dst_ref=finished,
+        send_sem=hsend.at[0],
+        recv_sem=hrecv.at[PASS, 0],
+        device_id=(s, dev_sib),
+        device_id_type=MESH,
+    ).wait_recv()
     for n in range(PIECES):
         for j in range(CHUNKS):
-            hop_arrived(FINAL + n, j)
             result_ref[n * PIECE : (n + 1) * PIECE, j * CW : (j + 1) * CW] = inbox[FINAL + n, j]
 
 
@@ -455,9 +464,9 @@
             pltpu.VMEM((KV_HEADS, LEN, 2 * HEAD_DIM), jnp.bfloat16),
             dma((4,)),
             dma((4,)),
-            dma((4, 11)),
+            dma((4, 8)),
             dma((1,)),
-            dma((STEPS + PIECES, CHUNKS)),
+            dma((PASS + 1, CHUNKS)),
         ],
         compiler_params=pltpu.CompilerParams(collective_id=0, has_side_effects=True),
     )(hidden_in, norm_gain, qkv_weight, qkv_bias, out_weight, rope, mask)

time: 172 us -> 171 us (level)
  no operation moved by 1% of the time
where the time goes in v6:
time: 171 us
  Pallas kernels  169 us (99%)
    pallas_call x1, Pallas kernels, per_device(): pl.pallas_call(kernel, name='sections', out_shape=jax.ShapeDtypeStruct((L...  169 us

profile of v6, /device:TPU:100, one launch (start us, length us, event | category | flops | bytes accessed | tf_op | source)
XLA Modules:
  0.0 171.0 jit_solution(2414415962131428233)
XLA Ops:
  0.0 169.4 %sections.1 = bf16[64,1536]{1,0:T(8,128)(2,1)} custom-call(bf16[8,1,64,1536]{3,2,1,0:T(8,128)(2,1)} %hidden_hbm.1, f32[2,1,1536]{2,1,0:T(1,128)} %gain_ref.1, bf16[2,1,96,2048]{3,2,1,0:T(8,128)(2,1)} %qkv_hbm.1, f32[2,1,2048]{2,1,0:T(1,128)} %bias_ref.1, bf16[2,1,96,1536]{3,2,1,0:T(8,128)(2,1)} %out_hbm.1, f32[2,4,32,128]{3,2,1,0:T(8,128)} %constant.4.clone.rope_ref, ...), custom_call_target="tpu_custom_call" | custom-call | tf_op jit(solution)/shard_map/sections/pallas_call | solution.py:451
  169.4 1.6 copy.9

commit v7 on v6

--- a/solution.py
+++ b/solution.py
@@ -231,12 +231,6 @@
     for t in range(4):
         own_copy(t).start()
 
-    @pl.when(s == 0)
-    def _():
-        for k in range(PASS):
-            for j in range(CHUNKS):
-                entering(k, j).start()
-
     crossing_in = (s == 4) | (s == 0)
     crossing_out = (s == 3) | (s == SECTIONS - 1)
     before = (lax.rem(s + SECTIONS - 1, SECTIONS), jnp.where(crossing_in, mirrored, f))
@@ -250,6 +244,13 @@
 
     gather_a(0)
     gather_a(1)
+
+    @pl.when(s == 0)
+    def _():
+        for k in range(PASS):
+            for j in range(CHUNKS):
+                entering(k, j).start()
+
     keys[...] = jnp.zeros_like(keys)
     values[...] = jnp.ones_like(values)
     gather_b(0)

time: 171 us -> 171 us (level)
  no operation moved by 1% of the time
where the time goes in v7:
time: 171 us
  Pallas kernels  169 us (99%)
    pallas_call x1, Pallas kernels, per_device(): pl.pallas_call(kernel, name='sections', out_shape=jax.ShapeDtypeStruct((L...  169 us

profile of v7, /device:TPU:100, one launch (start us, length us, event | category | flops | bytes accessed | tf_op | source)
XLA Modules:
  0.0 171.0 jit_solution(9207178223798405595)
XLA Ops:
  0.0 169.4 %sections.1 = bf16[64,1536]{1,0:T(8,128)(2,1)} custom-call(bf16[8,1,64,1536]{3,2,1,0:T(8,128)(2,1)} %hidden_hbm.1, f32[2,1,1536]{2,1,0:T(1,128)} %gain_ref.1, bf16[2,1,96,2048]{3,2,1,0:T(8,128)(2,1)} %qkv_hbm.1, f32[2,1,2048]{2,1,0:T(1,128)} %bias_ref.1, bf16[2,1,96,1536]{3,2,1,0:T(8,128)(2,1)} %out_hbm.1, f32[2,4,32,128]{3,2,1,0:T(8,128)} %constant.4.clone.rope_ref, ...), custom_call_target="tpu_custom_call" | custom-call | tf_op jit(solution)/shard_map/sections/pallas_call | solution.py:452
  169.4 1.6 copy.9
